TPU v7x, 32 devices: a whole 2x2x4 slice. The times are simulated.
32 devices in a mesh: lat: 8 (over y, x, core), lon: 4 (over z).
Axes of the slice: x: 2, y: 2, z: 4, core: 2. Of those that a mesh axis runs over, the one named last changes fastest.
Arguments:
- coeffs_old: float32 [640, 2, 3, 50, 640], P(('lat', 'lon')), may hold values from -0.16 to 0.16
- noise: bfloat16 [640, 2, 3, 50, 640], P(('lat', 'lon')), may hold values from -6 to 6
- legendre: float32 [640, 640, 640], P(('lat', 'lon')), may hold values from -0.25 to 0.25
- decay: float32 [3], replicated, may hold values from 0.3 to 0.97
- amplitude: float32 [3, 640], replicated, may hold values from 0.005 to 0.05
- wavenumber_of_slot: int32 [640], replicated, may hold values from 0 to 639, as said below
- lat_order: int32 [640], replicated, may hold values from 0 to 639, each once
Outputs:
- coeffs_new: float32 [640, 2, 3, 50, 640], P(('lat', 'lon'))
- pattern: float32 [640, 50, 1280], P(('lat', 'lon'))
Inputs may be any that keep to these rules, and one draw needn't show every extreme that they name: `wavenumber_of_slot`: every wavenumber fills exactly one slot; the sums of the wavenumbers of one device's 20 slots differ between devices by less than 32. `lat_order`: every latitude stands in exactly one row.
All inputs are finite; a program needn't handle non-finite values.
Results may differ from a plain program's by a relative error of at most 0.0003.
Values sent between devices are 32-bit elements; how exact they have to be, the bound alone decides.
A program may use at most 192 MiB of HBM per device.

v0:
```python
import jax
import jax.numpy as jnp
from jax import lax
from jax.sharding import PartitionSpec as P

LON = 1280
TWO_PI = 6.283185307179586


def evolve(coeffs_old, noise, decay, amplitude, waves):
    width = coeffs_old.shape[4]
    offsets = lax.broadcasted_iota(jnp.int32, (waves.shape[0], width), 1)
    live = waves[:, None] + offsets < width
    padded = jnp.concatenate([amplitude, jnp.zeros_like(amplitude)], axis=1)
    spread = jax.vmap(lambda wave: lax.dynamic_slice_in_dim(padded, wave, width, 1))(waves)
    factor = jnp.sqrt(1.0 - decay * decay)
    fresh = decay[None, None, :, None, None] * coeffs_old + (spread * factor[None, :, None])[
        :, None, :, None, :
    ] * noise.astype(jnp.float32)
    return jnp.where(live[:, None, None, None, :], fresh, jnp.zeros_like(fresh))


def synthesis_table(waves, length):
    column = lax.broadcasted_iota(jnp.int32, (waves.shape[0], length), 1)
    phase = waves[:, None] * column % length
    angle = phase.astype(jnp.float32) * (TWO_PI / length)
    weight = jnp.where(waves == 0, 1.0, 2.0).astype(jnp.float32)[:, None]
    return jnp.stack([weight * jnp.cos(angle), -weight * jnp.sin(angle)], axis=1)


def synthesize(values, table):
    return jnp.einsum("sreq,srl->qel", values, table, precision=lax.Precision.HIGHEST)


def local(coeffs_old, noise, legendre, decay, amplitude, wavenumber_of_slot, lat_order):
    lat_count = lax.axis_size("lat")
    lon_count = lax.axis_size("lon")
    lat_index = lax.axis_index("lat")
    lon_index = lax.axis_index("lon")
    slots = coeffs_old.shape[0]
    mine = lax.dynamic_slice_in_dim(
        wavenumber_of_slot, (lat_index * lon_count + lon_index) * slots, slots
    )
    coeffs_new = evolve(coeffs_old, noise, decay, amplitude, mine)
    field = jnp.einsum("srkej,slj->srel", coeffs_new, legendre, precision=lax.Precision.HIGHEST)
    field = jnp.take(field, lat_order, axis=3)
    ordered = wavenumber_of_slot.reshape(lat_count, lon_count, slots).transpose(1, 0, 2).reshape(-1)
    full_table = synthesis_table(ordered, LON)
    pattern = synthesize(
        lax.all_to_all(
            lax.all_to_all(field, "lat", split_axis=3, concat_axis=0, tiled=True),
            "lon",
            split_axis=3,
            concat_axis=0,
            tiled=True,
        ),
        full_table,
    )
    return (coeffs_new, pattern)


def solution(mesh):
    in_specs = (
        P(("lat", "lon"), None, None, None, None),
        P(("lat", "lon"), None, None, None, None),
        P(("lat", "lon"), None, None),
        P(),
        P(),
        P(),
        P(),
    )
    out_specs = (P(("lat", "lon"), None, None, None, None), P(("lat", "lon"), None, None))
    return jax.shard_map(local, mesh=mesh, in_specs=in_specs, out_specs=out_specs, check_vma=False)
```

profile of v0, /device:TPU:0, one launch (start us, length us, event | category | flops | bytes accessed | tf_op | source)
XLA Modules:
  0.0 590.6 jit_solution(11389839738425668350)
XLA Ops:
  2.0 0.8 fusion.12
  3.5 26.4 %while.1 = (s32[]{:T(128)}, f32[3,1280]{1,0:T(4,128)S(1)}, s32[20,2]{0,1:T(2,128)S(1)}, f32[20,3,640]{2,1,0:T(4,128)S(1)}, s32[]{:T(128)}) while((s32[]{:T(128)}, f32[3,1280]{1,0:T(4,128)S(1)}, s32[20,2]{0,1:T(2,128)S(1)}, f32[20,3,640]{2,1,0:T(4,128)S(1)}, s32[]{:T(128)}) %tuple.24), condition=%wide.while_cond, body=%wide.while_body.sunk | while | flops 2 | bytes 20585 | solution.py:15
  4.1 0.7 bitcast_dynamic-update-slice_fusion.2
  5.4 0.7 bitcast_dynamic-update-slice_fusion.2
  6.7 0.7 bitcast_dynamic-update-slice_fusion.2
  8.1 0.7 bitcast_dynamic-update-slice_fusion.2
  30.8 32.2 %fusion.15 = (f32[20,2,50,640]{3,1,2,0:T(2,128)}, f32[20,2,3,50,640]{4,1,3,2,0:T(2,128)}) fusion(bf16[20,2,3,50,640]{4,1,3,2,0:T(2,128)(2,1)} %param.8, f32[20,3,640]{2,1,0:T(4,128)S(1)} %broadcast_multiply_fusion, f32[20,2,3,50,640]{4,1,3,2,0:T(2,128)} %param.7, f32[3]{0:T(128)} %param.10, pred[20,640]{1,0:T(8,128)(4,1)S(1)} %add_compare_fusion), kind=kLoop, calls=%fused_computation.33 | loop fusion | flops 21760000 | bytes 43686412 | tf_op jit(solution)/shard_map/srkej,slj->srel/reduce_sum | solution.py:45
  63.0 36.1 %fusion = f32[20,2,50,640]{3,2,1,0:T(8,128)} fusion(f32[20,640,640]{2,1,0:T(8,128)} %param.9, f32[20,2,50,640]{3,1,2,0:T(2,128)} %get-tuple-element.18), kind=kOutput, calls=%fused_computation.3 | convolution fusion | flops 9830400000 | bytes 43008000 | tf_op jit(solution)/shard_map/srkej,slj->srel/dot_general | solution.py:45
  99.1 15.9 %copy.33 = f32[20,2,50,640]{2,1,3,0:T(2,128)} copy(f32[20,2,50,640]{3,2,1,0:T(8,128)} %fusion) | data formatting | bytes 10240000 | tf_op jit(solution)/shard_map/srkej,slj->srel/dot_general | solution.py:45
  115.0 38.6 %gather_fusion = f32[640,20,2,50]{3,2,1,0:T(2,128)} fusion(f32[20,2,50,640]{2,1,3,0:T(2,128)} %copy.33, s32[1024]{0:T(1024)S(1)} %pad_clamp_fusion), kind=kCustom, calls=%fused_computation | custom fusion | bytes 10242560 | tf_op jit(solution)/shard_map/jit(_take)/gather | solution.py:46
  153.6 10.2 %fusion.16 = f32[640,20,2,50]{3,2,1,0:T(2,128)} fusion(f32[640,20,2,50]{3,2,1,0:T(2,128)} %gather_fusion, pred[640]{0:T(1024)(128)(4,1)S(1)} %compare_and_fusion), kind=kLoop, calls=%fused_computation.34 | loop fusion | flops 1280000 | bytes 10240640
  163.8 27.8 %reshape.218 = f32[8,1,160000]{2,1,0:T(1,128)} reshape(f32[640,20,2,50]{3,2,1,0:T(2,128)} %fusion.16) | data formatting | bytes 10240000
  191.5 64.3 %all_to_all.36 = f32[8,1,160000]{2,1,0:T(1,128)} all-to-all(f32[8,1,160000]{2,1,0:T(1,128)} %reshape.218), channel_id=1, replica_groups=mesh['lat'=8,'lon'=4] {'lat'}, dimensions={0} | all-to-all | bytes 10240000 | tf_op jit(solution)/shard_map/all_to_all | solution.py:51
  256.3 17.0 %reduce = f32[8,160000]{1,0:T(8,128)} reduce(f32[8,1,160000]{2,1,0:T(1,128)} %all_to_all.36, f32[]{:T(128)} %broadcast.203), dimensions={1}, to_apply=%all_to_all.26.reduce_sub_computation | reduce | bytes 10240004 | tf_op jit(solution)/shard_map/all_to_all | solution.py:51
  273.3 33.3 %reshape.219 = f32[640,20,2,50]{3,2,1,0:T(2,128)} reshape(f32[8,160000]{1,0:T(8,128)} %reduce) | data formatting | bytes 10240000
  306.6 17.1 %copy.42 = f32[20,2,50,8,80]{4,3,1,2,0:T(8,128)} copy(f32[20,2,50,8,80]{2,1,0,4,3:T(2,128)} %bitcast.41) | data formatting | bytes 10240000 | tf_op jit(solution)/shard_map/all_to_all | solution.py:51
  323.7 13.0 %copy.35 = f32[8,20,2,50,80]{4,2,3,1,0:T(2,128)} copy(f32[8,20,2,50,80]{4,0,2,3,1:T(8,128)} %bitcast.43) | data formatting | bytes 10240000 | tf_op jit(solution)/shard_map/all_to_all | solution.py:51
  336.7 18.0 %copy.36 = f32[160,2,50,80]{0,1,2,3:T(2,128)} copy(f32[160,2,50,80]{3,1,2,0:T(2,128)} %bitcast.42) | data formatting | bytes 10240000 | tf_op jit(solution)/shard_map/all_to_all | solution.py:51
  354.7 5.7 all-to-all-start.1
  360.7 15.2 %cosine_multiply_fusion = (f32[640,1,1280]{2,0,1:T(8,128)S(1)}, f32[640,1,1280]{2,0,1:T(8,128)}) fusion(s32[640]{0:T(1024)S(1)} %reshape.185, f32[640]{0:T(1024)S(1)} %get-tuple-element.24, f32[640]{0:T(1024)S(1)} %get-tuple-element.25), kind=kLoop, calls=%fused_computation.17 | loop fusion | flops 9011200 | bytes 6561280 | tf_op jit(solution)/shard_map/mul | solution.py:28
  375.9 164.0 %all-to-all-done.1 = f32[160,2,50,80]{0,1,2,3:T(2,128)} async-done(((f32[160,2,50,80]{0,1,2,3:T(2,128)}), f32[160,2,50,80]{0,1,2,3:T(2,128)}, u32[]{:S(2)}, u32[]{:S(2)}) %all-to-all-start.1) | async-done | bytes 5120032 | tf_op jit(solution)/shard_map/all_to_all | solution.py:50
  539.9 11.8 %copy.44 = f32[4,160,2,50,20]{1,0,3,2,4:T(4,128)} copy(f32[4,160,2,50,20]{1,2,3,4,0:T(2,128)} %bitcast.11) | data formatting | bytes 10240000 | tf_op jit(solution)/shard_map/all_to_all | solution.py:50
  551.7 9.5 %reshape.217 = f32[640,2,50,20]{0,2,1,3:T(8,128)} reshape(f32[4,160,2,50,20]{1,0,3,2,4:T(4,128)} %copy.44) | data formatting | bytes 10240000 | tf_op jit(solution)/shard_map/all_to_all | solution.py:50
  561.3 29.1 %fusion.6 = f32[20,50,1280]{2,1,0:T(8,128)} fusion(f32[640,2,50,20]{0,2,1,3:T(8,128)} %reshape.217, f32[640,1,1280]{2,0,1:T(8,128)} %get-tuple-element.23, f32[640,1,1280]{2,0,1:T(8,128)S(1)} %get-tuple-element.22), kind=kOutput, calls=%fused_computation.13 | convolution fusion | flops 19662438400 | bytes 16793600 | tf_op jit(solution)/shard_map/sreq,srl->qel/dot_general | solution.py:32
  (72 shorter events, 27.2 us)
Async XLA Ops:
  354.7 5.8 copy-start
  354.7 185.2 %all-to-all-start.1 = ((f32[160,2,50,80]{0,1,2,3:T(2,128)}), f32[160,2,50,80]{0,1,2,3:T(2,128)}, u32[]{:S(2)}, u32[]{:S(2)}) async-start(f32[160,2,50,80]{0,1,2,3:T(2,128)} %copy.36), calls=%async_computation.1 | async-start | bytes 16384000 | tf_op jit(solution)/shard_map/all_to_all | solution.py:50
where the time goes:
time: 601 us; the launch traced here: 591 us
  local copies, waits for them, and re-layouts  213 us (35%)
  waiting for transfers between devices  164 us (27%)
  other arithmetic  77.6 us (13%)
  matrix products  65.2 us (11%)
  blocking collectives  64.3 us (11%)
    all_to_all x1, waiting for transfers between devices, local(): lax.all_to_all(lax.all_to_all(field, 'lat', split_axis=3, concat_axis=0,...  164 us
    all_to_all x1, blocking collectives, local(): lax.all_to_all(field, 'lat', split_axis=3, concat_axis=0, tiled=True)  64.3 us
    unnamed x4, local copies, waits for them, and re-layouts  61.1 us
    all_to_all x4, local copies, waits for them, and re-layouts, local(): lax.all_to_all(field, 'lat', split_axis=3, concat_axis=0, tiled=True)  48.6 us
    gather x1, local copies, waits for them, and re-layouts, local(): field = jnp.take(field, lat_order, axis=3)  38.6 us
    dot_general x1, matrix products, local(): jnp.einsum('srkej,slj->srel', coeffs_new, legendre, precision=lax.Precisi...  36.1 us
    reduce_sum x1, other arithmetic, local(): jnp.einsum('srkej,slj->srel', coeffs_new, legendre, precision=lax.Precisi...  32.2 us
    dot_general x1, matrix products, synthesize(): jnp.einsum('sreq,srl->qel', values, table, precision=lax.Precision.HIGHEST)  29.1 us
  transfers between devices with their start and end apart: 1, of which 1 were waited for; matrix products, arithmetic and copies ran while one was open for 3% of the time, Pallas kernels for 0%

commit v1 on v0

--- a/solution.py
+++ b/solution.py
@@ -5,6 +5,24 @@
 
 LON = 1280
 TWO_PI = 6.283185307179586
+
+
+def scan_pieces_all_here(load):
+    seen_now = jax.lax.psum(1, "lon")
+    raw_out = jax.lax.axis_index("lon")
+    x_now, latest = (seen_now, raw_out)
+    known = load.shape[3] // x_now
+    z2 = list(load.shape)
+    z2[3] = known
+    h_now = z2[0]
+    z2[0] = h_now * x_now
+    tmp = jnp.zeros(z2, load.dtype)
+    for d in range(x_now):
+        top = lax.dynamic_slice_in_dim(load, (latest ^ d) * known, known, axis=3)
+        if d:
+            top = jax.lax.ppermute(top, "lon", [(hop_no, hop_no ^ d) for hop_no in range(x_now)])
+        tmp = lax.dynamic_update_slice_in_dim(tmp, top, (latest ^ d) * h_now, axis=0)
+    return tmp
 
 
 def evolve(coeffs_old, noise, decay, amplitude, waves):
@@ -47,13 +65,7 @@
     ordered = wavenumber_of_slot.reshape(lat_count, lon_count, slots).transpose(1, 0, 2).reshape(-1)
     full_table = synthesis_table(ordered, LON)
     pattern = synthesize(
-        lax.all_to_all(
-            lax.all_to_all(field, "lat", split_axis=3, concat_axis=0, tiled=True),
-            "lon",
-            split_axis=3,
-            concat_axis=0,
-            tiled=True,
-        ),
+        scan_pieces_all_here(lax.all_to_all(field, "lat", split_axis=3, concat_axis=0, tiled=True)),
         full_table,
     )
     return (coeffs_new, pattern)

time: 601 us -> 638 us (1.062)
  the two profiles are of different devices: /device:TPU:0 before, /device:TPU:18 now
where the time goes in v1:
time: 638 us; the launch traced here: 627 us
  local copies, waits for them, and re-layouts  327 us (51%)
  waiting for transfers between devices  144 us (23%)
  other arithmetic  78.1 us (12%)
  matrix products  68.2 us (11%)
  starting transfers between devices  8.54 us (1%)
    dynamic_slice x5, local copies, waits for them, and re-layouts, scan_pieces_all_here(): top = lax.dynamic_slice_in_dim(load, (latest ^ d) * known, known, axis=3)  87.4 us
    ppermute x3, waiting for transfers between devices, scan_pieces_all_here(): jax.lax.ppermute(top, 'lon', [(hop_no, hop_no ^ d) for hop_no in range(x_...  86.5 us
    unnamed x4, local copies, waits for them, and re-layouts  61.3 us
    all_to_all x1, waiting for transfers between devices, local(): lax.all_to_all(field, 'lat', split_axis=3, concat_axis=0, tiled=True)  57.6 us
    dynamic_update_slice x4, local copies, waits for them, and re-layouts, scan_pieces_all_here(): lax.dynamic_update_slice_in_dim(tmp, top, (latest ^ d) * h_now, axis=0)  56.9 us
    gather x1, local copies, waits for them, and re-layouts, local(): field = jnp.take(field, lat_order, axis=3)  38.6 us
    dot_general x1, matrix products, local(): jnp.einsum('srkej,slj->srel', coeffs_new, legendre, precision=lax.Precisi...  36.1 us
    reduce_sum x1, other arithmetic, local(): jnp.einsum('srkej,slj->srel', coeffs_new, legendre, precision=lax.Precisi...  32.3 us
  transfers between devices with their start and end apart: 4, of which 3 were waited for; matrix products, arithmetic and copies ran while one was open for 16% of the time, Pallas kernels for 0%

profile of v1, /device:TPU:18, one launch (start us, length us, event | category | flops | bytes accessed | tf_op | source)
XLA Modules:
  0.0 626.6 jit_solution(9082055295321734505)
XLA Ops:
  3.5 26.4 %while.1 = (s32[]{:T(128)}, f32[3,1280]{1,0:T(4,128)S(1)}, s32[20,2]{0,1:T(2,128)S(1)}, f32[20,3,640]{2,1,0:T(4,128)S(1)}, s32[]{:T(128)}) while((s32[]{:T(128)}, f32[3,1280]{1,0:T(4,128)S(1)}, s32[20,2]{0,1:T(2,128)S(1)}, f32[20,3,640]{2,1,0:T(4,128)S(1)}, s32[]{:T(128)}) %tuple.27), condition=%wide.while_cond, body=%wide.while_body.sunk | while | flops 2 | bytes 20577 | solution.py:33
  30.8 32.3 %fusion.15 = (f32[20,2,50,640]{3,1,2,0:T(2,128)}, f32[20,2,3,50,640]{4,1,3,2,0:T(2,128)}) fusion(bf16[20,2,3,50,640]{4,1,3,2,0:T(2,128)(2,1)} %param.8, f32[20,3,640]{2,1,0:T(4,128)S(1)} %broadcast_multiply_fusion, f32[20,2,3,50,640]{4,1,3,2,0:T(2,128)} %param.7, f32[3]{0:T(128)} %param.10, pred[20,640]{1,0:T(8,128)(4,1)S(1)} %add_compare_fusion), kind=kLoop, calls=%fused_computation.37 | loop fusion | flops 21760000 | bytes 43686412 | tf_op jit(solution)/shard_map/srkej,slj->srel/reduce_sum | solution.py:63
  63.0 36.1 %fusion = f32[20,2,50,640]{3,2,1,0:T(8,128)} fusion(f32[20,640,640]{2,1,0:T(8,128)} %param.9, f32[20,2,50,640]{3,1,2,0:T(2,128)} %get-tuple-element.18), kind=kOutput, calls=%fused_computation.3 | convolution fusion | flops 9830400000 | bytes 43008000 | tf_op jit(solution)/shard_map/srkej,slj->srel/dot_general | solution.py:63
  99.1 15.9 %copy.27 = f32[20,2,50,640]{2,1,3,0:T(2,128)} copy(f32[20,2,50,640]{3,2,1,0:T(8,128)} %fusion) | data formatting | bytes 10240000 | tf_op jit(solution)/shard_map/srkej,slj->srel/dot_general | solution.py:63
  115.0 38.6 %gather_fusion = f32[640,20,2,50]{3,2,1,0:T(2,128)} fusion(f32[20,2,50,640]{2,1,3,0:T(2,128)} %copy.27, s32[1024]{0:T(1024)S(1)} %pad_clamp_fusion), kind=kCustom, calls=%fused_computation | custom fusion | bytes 10242560 | tf_op jit(solution)/shard_map/jit(_take)/gather | solution.py:64
  163.8 27.8 %reshape.217 = f32[8,1,160000]{2,1,0:T(1,128)} reshape(f32[640,20,2,50]{3,2,1,0:T(2,128)} %fusion.16) | data formatting | bytes 10240000
  196.6 57.6 %all-to-all-done = f32[8,1,160000]{2,1,0:T(1,128)} async-done(((f32[8,1,160000]{2,1,0:T(1,128)}), f32[8,1,160000]{2,1,0:T(1,128)}, u32[]{:S(2)}, u32[]{:S(2)}) %all-to-all-start) | async-done | bytes 5120032 | tf_op jit(solution)/shard_map/all_to_all | solution.py:68
  254.7 16.8 %reduce = f32[8,160000]{1,0:T(8,128)} reduce(f32[8,1,160000]{2,1,0:T(1,128)} %all-to-all-done, f32[]{:T(128)} %broadcast.203), dimensions={1}, to_apply=%all_to_all.13.reduce_sub_computation | reduce | bytes 10240004 | tf_op jit(solution)/shard_map/all_to_all | solution.py:68
  271.5 33.5 %reshape.218 = f32[640,20,2,50]{3,2,1,0:T(2,128)} reshape(f32[8,160000]{1,0:T(8,128)} %reduce) | data formatting | bytes 10240000
  305.0 17.1 %copy.39 = f32[20,2,50,8,80]{4,3,1,2,0:T(8,128)} copy(f32[20,2,50,8,80]{2,1,0,4,3:T(2,128)} %bitcast.37) | data formatting | bytes 10240000 | tf_op jit(solution)/shard_map/all_to_all | solution.py:68
  322.1 12.0 %copy.29 = f32[8,20,2,50,80]{4,2,3,1,0:T(2,128)S(1)} copy(f32[8,20,2,50,80]{4,0,2,3,1:T(8,128)} %bitcast.38) | data formatting | bytes 10240000 | tf_op jit(solution)/shard_map/all_to_all | solution.py:68
  334.1 36.3 %constant_dynamic-slice_fusion.1 = (f32[160,2,50,20]{3,1,2,0:T(2,128)}, f32[160,2,50,20]{3,1,2,0:T(2,128)}, f32[160,2,50,20]{3,1,2,0:T(2,128)}, f32[160,2,50,20]{3,1,2,0:T(2,128)}) fusion(f32[160,2,50,80]{3,1,2,0:T(2,128)S(1)} %bitcast.36, s32[]{:T(128)S(6)} %select_n.85, s32[]{:T(128)S(6)} %select_n.83, s32[]{:T(128)S(6)} %select_n.81, s32[]{:T(128)S(6)} %select_n.79), kind=kLoop, calls=%fused_computation.29 | loop fusion | bytes 10240016 | tf_op jit(solution)/shard_map/dynamic_slice | solution.py:21
  370.4 13.1 %copy.31 = f32[160,2,50,20]{0,1,3,2:T(2,128)} copy(f32[160,2,50,20]{3,1,2,0:T(2,128)} %get-tuple-element.24) | data formatting | bytes 2560000 | tf_op jit(solution)/shard_map/dynamic_slice | solution.py:21
  385.0 13.0 %copy.33 = f32[160,2,50,20]{0,1,3,2:T(2,128)} copy(f32[160,2,50,20]{3,1,2,0:T(2,128)} %get-tuple-element.23) | data formatting | bytes 2560000 | tf_op jit(solution)/shard_map/dynamic_slice | solution.py:21
  398.4 13.1 %copy.35 = f32[160,2,50,20]{0,1,3,2:T(2,128)} copy(f32[160,2,50,20]{3,1,2,0:T(2,128)} %get-tuple-element.22) | data formatting | bytes 2560000 | tf_op jit(solution)/shard_map/dynamic_slice | solution.py:21
  413.3 15.9 %cosine_multiply_fusion = (f32[640,1,1280]{2,0,1:T(8,128)}, f32[640,1,1280]{2,0,1:T(8,128)}) fusion(s32[640]{0:T(1024)S(1)} %reshape.185, f32[640]{0:T(1024)S(1)} %get-tuple-element.28, f32[640]{0:T(1024)S(1)} %get-tuple-element.29), kind=kLoop, calls=%fused_computation.17 | loop fusion | flops 9011200 | bytes 6561280 | tf_op jit(solution)/shard_map/mul | solution.py:46
  429.2 12.0 %copy.30 = f32[160,2,50,20]{0,2,1,3:T(8,128)S(1)} copy(f32[160,2,50,20]{3,1,2,0:T(2,128)} %get-tuple-element.25) | data formatting | bytes 2560000 | tf_op jit(solution)/shard_map/dynamic_slice | solution.py:21
  444.1 15.8 %dynamic_update_slice.12 = f32[640,2,50,20]{0,2,1,3:T(8,128)} dynamic-update-slice(f32[640,2,50,20]{0,2,1,3:T(8,128)} %broadcast_in_dim.49, f32[160,2,50,20]{0,2,1,3:T(8,128)S(1)} %copy.30, s32[]{:T(128)S(6)} %select_n.80, s32[]{:T(128)} %constant.24.clone.1, s32[]{:T(128)} %constant.24.clone.1, s32[]{:T(128)} %constant.24.clone.1) | dynamic-update-slice | bytes 2560004 | tf_op jit(solution)/shard_map/dynamic_update_slice | solution.py:24
  462.1 15.0 %dynamic_update_slice.13 = f32[640,2,50,20]{0,2,1,3:T(8,128)} dynamic-update-slice(f32[640,2,50,20]{0,2,1,3:T(8,128)} %dynamic_update_slice.12, f32[160,2,50,20]{0,2,1,3:T(8,128)S(1)} %copy.32, s32[]{:T(128)S(6)} %select_n.82, s32[]{:T(128)} %constant.24.clone.1, s32[]{:T(128)} %constant.24.clone.1, s32[]{:T(128)} %constant.24.clone.1) | dynamic-update-slice | bytes 2560004 | tf_op jit(solution)/shard_map/dynamic_update_slice | solution.py:24
  477.1 54.4 %collective-permute-done.1 = f32[160,2,50,20]{0,1,3,2:T(2,128)} collective-permute-done((f32[160,2,50,20]{0,1,3,2:T(2,128)}, f32[160,2,50,20]{0,1,3,2:T(2,128)}, u32[]{:S(2)}, u32[]{:S(2)}) %collective-permute-start.1) | collective-permute-done | bytes 1280032 | tf_op jit(solution)/shard_map/ppermute | solution.py:23
  533.7 10.4 %dynamic_update_slice.14 = f32[640,2,50,20]{0,2,1,3:T(8,128)} dynamic-update-slice(f32[640,2,50,20]{0,2,1,3:T(8,128)} %dynamic_update_slice.13, f32[160,2,50,20]{0,2,1,3:T(8,128)S(1)} %copy.34, s32[]{:T(128)S(6)} %select_n.84, s32[]{:T(128)} %constant.24.clone.1, s32[]{:T(128)} %constant.24.clone.1, s32[]{:T(128)} %constant.24.clone.1) | dynamic-update-slice | bytes 2560004 | tf_op jit(solution)/shard_map/dynamic_update_slice | solution.py:24
  544.1 32.1 %collective-permute-done.2 = f32[160,2,50,20]{0,1,3,2:T(2,128)} collective-permute-done((f32[160,2,50,20]{0,1,3,2:T(2,128)}, f32[160,2,50,20]{0,1,3,2:T(2,128)}, u32[]{:S(2)}, u32[]{:S(2)}) %collective-permute-start.2) | collective-permute-done | bytes 1280032 | tf_op jit(solution)/shard_map/ppermute | solution.py:23
  578.5 15.8 %dynamic_update_slice.15 = f32[640,2,50,20]{0,2,1,3:T(8,128)} dynamic-update-slice(f32[640,2,50,20]{0,2,1,3:T(8,128)} %dynamic_update_slice.14, f32[160,2,50,20]{0,2,1,3:T(8,128)S(1)} %copy.36, s32[]{:T(128)S(6)} %select_n.86, s32[]{:T(128)} %constant.24.clone.1, s32[]{:T(128)} %constant.24.clone.1, s32[]{:T(128)} %constant.24.clone.1) | dynamic-update-slice | bytes 2560004 | tf_op jit(solution)/shard_map/dynamic_update_slice | solution.py:24
  594.3 32.1 %fusion.6 = f32[20,50,1280]{2,1,0:T(8,128)} fusion(f32[640,2,50,20]{0,2,1,3:T(8,128)} %dynamic_update_slice.15, f32[640,1,1280]{2,0,1:T(8,128)} %get-tuple-element.27, f32[640,1,1280]{2,0,1:T(8,128)} %get-tuple-element.26), kind=kOutput, calls=%fused_computation.13 | convolution fusion | flops 19662438400 | bytes 16793600 | tf_op jit(solution)/shard_map/sreq,srl->qel/dot_general | solution.py:50
  (87 shorter events, 59.2 us)
Async XLA Ops:
  191.5 62.7 %all-to-all-start = ((f32[8,1,160000]{2,1,0:T(1,128)}), f32[8,1,160000]{2,1,0:T(1,128)}, u32[]{:S(2)}, u32[]{:S(2)}) async-start(f32[8,1,160000]{2,1,0:T(1,128)} %reshape.217), calls=%async_computation | async-start | bytes 10240000 | tf_op jit(solution)/shard_map/all_to_all | solution.py:68
  383.4 76.4 %collective-permute-start = (f32[160,2,50,20]{0,1,3,2:T(2,128)}, f32[160,2,50,20]{0,1,3,2:T(2,128)}, u32[]{:S(2)}, u32[]{:S(2)}) collective-permute-start(f32[160,2,50,20]{0,1,3,2:T(2,128)} %copy.31), channel_id=1, source_target_pairs={{0,1},{1,0},{2,3},{3,2},{4,5},{5,4},{6,7},{7,6},{8,9},{9,8},{10,11... | collective-permute-start | bytes 3840008 | tf_op jit(solution)/shard_map/ppermute | solution.py:23
  398.1 15.0 %copy-start = (s32[640]{0:T(1024)S(1)}, s32[640]{0:T(1024)}, u32[]{:S(2)}) copy-start(s32[640]{0:T(1024)} %param.12) | copy-start | bytes 7684
  398.1 133.4 %collective-permute-start.1 = (f32[160,2,50,20]{0,1,3,2:T(2,128)}, f32[160,2,50,20]{0,1,3,2:T(2,128)}, u32[]{:S(2)}, u32[]{:S(2)}) collective-permute-start(f32[160,2,50,20]{0,1,3,2:T(2,128)} %copy.33), channel_id=1, source_target_pairs={{0,2},{1,3},{2,0},{3,1},{4,6},{5,7},{6,4},{7,5},{8,10},{9,11},{10,... | collective-permute-start | bytes 3840008 | tf_op jit(solution)/shard_map/ppermute | solution.py:23
  411.5 164.8 %collective-permute-start.2 = (f32[160,2,50,20]{0,1,3,2:T(2,128)}, f32[160,2,50,20]{0,1,3,2:T(2,128)}, u32[]{:S(2)}, u32[]{:S(2)}) collective-permute-start(f32[160,2,50,20]{0,1,3,2:T(2,128)} %copy.35), channel_id=1, source_target_pairs={{0,3},{1,2},{2,1},{3,0},{4,7},{5,6},{6,5},{7,4},{8,11},{9,10},{10,... | collective-permute-start | bytes 3840008 | tf_op jit(solution)/shard_map/ppermute | solution.py:23
